TPU v7x, 512 devices: a whole 4x4x16 slice. The times are simulated.
512 devices in a mesh: seq: 64 (over z, y_lo, core), head: 8 (over y_hi, x).
Axes of the slice: x: 4, y: 4 (y_hi: 2, y_lo: 2; y = y_hi * 2 + y_lo), z: 16, core: 2. Of those that a mesh axis runs over, the one named last changes fastest.
Arguments:
- q_main: bfloat16 [8192, 128, 576], P('seq', 'head'), may hold values from -6 to 6
- latent_keys: bfloat16 [8192, 576], P('seq'), may hold values from -6 to 6
- lse_main: float32 [8192, 128], P('seq', 'head'), may hold values from 0.5 to 2.5
- index_queries: bfloat16 [8192, 64, 128], P('seq', 'head'), may hold values from -6 to 6
- index_weights: float32 [8192, 64], P('seq', 'head'), may hold values from -1.5 to 1.5
- index_keys: bfloat16 [8192, 128], P('seq'), may hold values from -6 to 6
- lse_index: float32 [8192], P('seq'), may hold values from 0 to 2
- slab_order: int32 [64], replicated, may hold values from 0 to 63, each once
- block_live: int32 [64, 64], replicated, may hold values 0 or 1
Outputs:
- key_grad: float32 [8192, 128], P('seq')
Inputs may be any that keep to these rules, and one draw needn't show every extreme that they name: `slab_order`: a permutation: every slab number once.
All inputs are finite; a program needn't handle non-finite values.
Results may differ from a plain program's by a relative error of at most 0.0028.
Values may be sent and summed in bfloat16 or wider, within the bound.
A program may use at most 64 MiB of HBM per device.

v0:
```python
import jax
import jax.numpy as jnp
from jax import lax
from jax.sharding import PartitionSpec as P

HEADS = 128
HOPS = 8


main_scale = 1.0 / 192.0**0.5


def passed_along(block, axis, distance):
    devices = range(lax.axis_size(axis))
    route = [((i - distance) % len(devices), i) for i in devices]
    return lax.ppermute(block, axis, route)


def copy_for_each(value, axis):
    length = lax.axis_size(axis)
    return lax.all_to_all(
        jnp.broadcast_to(value[None], (length, *value.shape)), axis, 0, 0, tiled=True
    )


def over_copies(value, axis):
    return copy_for_each(value, axis).sum(axis=0)


def in_one(arrays, axis):
    ends = [0]
    for a in arrays:
        ends.append(ends[-1] + a.size)
    subtotal = over_copies(jnp.concatenate([a.ravel() for a in arrays]), axis)
    return tuple((subtotal[b:e].reshape(a.shape) for a, b, e in zip(arrays, ends, ends[1:])))


def pick_entry(table, positions, wanted):
    return jnp.sum(jnp.where(positions == wanted, table, 0))


def local(
    q_main,
    latent_keys,
    lse_main,
    index_queries,
    index_weights,
    index_keys,
    lse_index,
    slab_order,
    block_live,
):
    seq_count = lax.axis_size("seq")
    seq_place = lax.axis_index("seq")
    block_rows = latent_keys.shape[0]
    heads_here = q_main.shape[1]
    index_here = index_queries.shape[1]
    index_width = index_keys.shape[1]
    index_scale = 1.0 / index_width**0.5
    positions = jnp.arange(seq_count, dtype=jnp.int32)
    within = jnp.arange(block_rows, dtype=jnp.int32)
    own_slab = pick_entry(slab_order, positions, seq_place)
    live_table = jnp.sum(jnp.where((positions == own_slab)[:, None], block_live, 0), axis=0)
    query_spots = own_slab * block_rows + within
    query_flat = q_main.reshape(block_rows * heads_here, q_main.shape[2])
    index_flat = index_queries.reshape(block_rows * index_here, index_width)

    def tile_terms(latent_block, key_block):
        scores = jnp.einsum(
            "ac,bc->ab", query_flat, latent_block, preferred_element_type=jnp.float32
        )
        scores = scores.reshape(block_rows, heads_here, block_rows) * main_scale
        head_mass = jnp.sum(jnp.exp(scores - lse_main[:, :, None]), axis=1)
        relu_input = jnp.einsum(
            "ac,bc->ab", index_flat, key_block, preferred_element_type=jnp.float32
        )
        relu_input = relu_input.reshape(block_rows, index_here, block_rows) * index_scale
        logits = jnp.sum(index_weights[:, :, None] * jnp.maximum(relu_input, 0.0), axis=1)
        return (head_mass, logits, relu_input)

    def empty_terms(latent_block, key_block):
        square = jnp.zeros((block_rows, block_rows), jnp.float32)
        return (square, square, jnp.zeros((block_rows, index_here, block_rows), jnp.float32))

    def key_terms(grad_tile, relu_input):
        weighted = jnp.where(
            relu_input > 0.0, grad_tile[:, None, :] * index_weights[:, :, None], 0.0
        ).astype(jnp.bfloat16)
        summed = lax.dot_general(
            weighted.reshape(block_rows * index_here, block_rows),
            index_flat,
            (((0,), (0,)), ((), ())),
            preferred_element_type=jnp.float32,
        )
        return summed * index_scale

    def empty_keys(grad_tile, relu_input):
        return jnp.zeros((block_rows, index_width), jnp.float32)

    latent_block, key_block = (latent_keys, index_keys)
    carried = jnp.zeros((block_rows, index_width), jnp.float32)
    for cycle_step in range(HOPS):
        if cycle_step > 0:
            latent_block, key_block = passed_along((latent_block, key_block), "seq", 1)
        source = (seq_place - cycle_step) % seq_count
        key_slab = pick_entry(slab_order, positions, source)
        key_spots = key_slab * block_rows + within
        allowed = pick_entry(live_table, positions, key_slab)
        live_mask = (key_spots[None, :] <= query_spots[:, None]) & (allowed == 1)
        any_live = jnp.any(live_mask)
        head_mass, logits, relu_input = lax.cond(
            any_live, tile_terms, empty_terms, latent_block, key_block
        )
        head_mass, logits = in_one((head_mass, logits), "head")
        grad_tile = jnp.where(
            live_mask, jnp.exp(logits - lse_index[:, None]) - head_mass / HEADS, 0.0
        )
        contrib = lax.cond(any_live, key_terms, empty_keys, grad_tile, relu_input)
        if cycle_step > 0:
            carried = passed_along(carried, "seq", 1)
        carried = carried + contrib
    key_total = passed_along(carried, "seq", 1 - HOPS)
    return over_copies(key_total, "head")


def solution(mesh):
    placed = (
        P("seq", "head", None),
        P("seq", None),
        P("seq", "head"),
        P("seq", "head", None),
        P("seq", "head"),
        P("seq", None),
        P("seq"),
        P(),
        P(),
    )
    return jax.shard_map(
        local, mesh=mesh, in_specs=placed, out_specs=P("seq", None), check_vma=False
    )
```

profile of v0, /device:TPU:65, one launch (start us, length us, event | category | flops | bytes accessed | tf_op | source)
XLA Modules:
  0.0 295.3 jit_solution(3317888952291090953)
XLA Ops:
  8.7 5.7 %fusion.112 = (s32[]{:T(128)}, s32[]{:T(128)}, s32[]{:T(128)}, s32[]{:T(128)}, s32[]{:T(128)}, /*index=5*/s32[]{:T(128)}, s32[]{:T(128)}, s32[]{:T(128)}) fusion(s32[64]{0:T(128)S(1)} %select_reduce_fusion, s32[]{:T(128)} %get-tuple-element.765, s32[]{:T(128)} %get-tuple-element.773, s32[]{:T(128)} %get-tuple-element.766, s32[]{:T(128)} %get-tuple-element.767, ...), kind=kLoop, calls=%fused_computation.202 | loop fusion | flops 1528 | bytes 320 | tf_op jit(solution)/shard_map/reduce_sum | solution.py:39
  29.9 6.7 %all-to-all-start = ((f32[8,1,32768]{2,1,0:T(1,128)}), f32[8,1,32768]{2,1,0:T(1,128)}, u32[]{:S(2)}, u32[]{:S(2)}) async-start(f32[8,1,32768]{2,1,0:T(1,128)} %broadcast_in_dim.93), calls=%async_computation | async-start | bytes 2097152 | tf_op jit(solution)/shard_map/all_to_all | solution.py:21
  43.1 7.5 %collective-permute-done.1 = bf16[128,128]{1,0:T(8,128)(2,1)} collective-permute-done((bf16[128,128]{1,0:T(8,128)(2,1)S(1)}, bf16[128,128]{1,0:T(8,128)(2,1)}, u32[]{:S(2)}, u32[]{:S(2)}) %collective-permute-start.1) | collective-permute-done | bytes 32800 | tf_op jit(solution)/shard_map/ppermute | solution.py:16
  54.7 4.6 %all-to-all-start.1 = ((f32[8,1,32768]{2,1,0:T(1,128)}), f32[8,1,32768]{2,1,0:T(1,128)}, u32[]{:S(2)}, u32[]{:S(2)}) async-start(f32[8,1,32768]{2,1,0:T(1,128)} %broadcast_in_dim.97), calls=%async_computation.1 | async-start | bytes 2097152 | tf_op jit(solution)/shard_map/all_to_all | solution.py:21
  59.4 8.1 %collective-permute-start.5 = (bf16[128,576]{1,0:T(8,128)(2,1)}, bf16[128,576]{1,0:T(8,128)(2,1)S(1)}, u32[]{:S(2)}, u32[]{:S(2)}) collective-permute-start(bf16[128,576]{1,0:T(8,128)(2,1)} %copy-done.12), channel_id=1, source_target_pairs={{504,0},{0,8},{8,16},{16,24},{24,32},{32,40},{40,48},{48,56},{56,6... | collective-permute-start | bytes 442376 | tf_op jit(solution)/shard_map/ppermute | solution.py:16
  70.1 4.6 %collective-permute-done.4 = bf16[128,128]{1,0:T(8,128)(2,1)S(1)} collective-permute-done((bf16[128,128]{1,0:T(8,128)(2,1)}, bf16[128,128]{1,0:T(8,128)(2,1)S(1)}, u32[]{:S(2)}, u32[]{:S(2)}) %collective-permute-start.4) | collective-permute-done | bytes 32800 | tf_op jit(solution)/shard_map/ppermute | solution.py:16
  78.5 4.9 %all-to-all-start.2 = ((f32[8,1,32768]{2,1,0:T(1,128)}), f32[8,1,32768]{2,1,0:T(1,128)}, u32[]{:S(2)}, u32[]{:S(2)}) async-start(f32[8,1,32768]{2,1,0:T(1,128)} %broadcast_in_dim.98), calls=%async_computation.2 | async-start | bytes 2097152 | tf_op jit(solution)/shard_map/all_to_all | solution.py:21
  89.9 8.7 %collective-permute-done.7 = bf16[128,128]{1,0:T(8,128)(2,1)} collective-permute-done((bf16[128,128]{1,0:T(8,128)(2,1)S(1)}, bf16[128,128]{1,0:T(8,128)(2,1)}, u32[]{:S(2)}, u32[]{:S(2)}) %collective-permute-start.7) | collective-permute-done | bytes 32800 | tf_op jit(solution)/shard_map/ppermute | solution.py:16
  113.2 8.1 %collective-permute-done.10 = bf16[128,128]{1,0:T(8,128)(2,1)S(1)} collective-permute-done((bf16[128,128]{1,0:T(8,128)(2,1)}, bf16[128,128]{1,0:T(8,128)(2,1)S(1)}, u32[]{:S(2)}, u32[]{:S(2)}) %collective-permute-start.10) | collective-permute-done | bytes 32800 | tf_op jit(solution)/shard_map/ppermute | solution.py:16
  122.0 4.8 %conditional.24 = (f32[128,8,128]{2,1,0:T(8,128)}, f32[16384]{0:T(1024)S(1)}, f32[16384]{0:T(1024)S(1)}) conditional(s32[]{:T(128)} %convert_element_type.60, () %tuple.166, (bf16[1024,128]{1,0:T(8,128)(2,1)}, bf16[128,128]{1,0:T(8,128)(2,1)S(1)}, bf16[2048,576]{1,0:T(8,128)(2,1)S(1)}, bf16[128,576]{1,0:T(8,128)(2,1)S(1)}, ...), branch_computations={%region_45.46_spmd, %region_46.49_spmd} | conditional | flops 336822272 | bytes 4083764 | solution.py:111
  128.3 6.0 %all-to-all-start.4 = ((f32[8,1,32768]{2,1,0:T(1,128)}), f32[8,1,32768]{2,1,0:T(1,128)}, u32[]{:S(2)}, u32[]{:S(2)}) async-start(f32[8,1,32768]{2,1,0:T(1,128)} %broadcast_in_dim.100), calls=%async_computation.4 | async-start | bytes 2097152 | tf_op jit(solution)/shard_map/all_to_all | solution.py:21
  140.9 8.2 %collective-permute-done.13 = bf16[128,128]{1,0:T(8,128)(2,1)} collective-permute-done((bf16[128,128]{1,0:T(8,128)(2,1)S(1)}, bf16[128,128]{1,0:T(8,128)(2,1)}, u32[]{:S(2)}, u32[]{:S(2)}) %collective-permute-start.13) | collective-permute-done | bytes 32800 | tf_op jit(solution)/shard_map/ppermute | solution.py:16
  157.5 7.2 %collective-permute-start.17 = (bf16[128,576]{1,0:T(8,128)(2,1)}, bf16[128,576]{1,0:T(8,128)(2,1)S(1)}, u32[]{:S(2)}, u32[]{:S(2)}) collective-permute-start(bf16[128,576]{1,0:T(8,128)(2,1)} %collective-permute-done.14), channel_id=1, source_target_pairs={{504,0},{0,8},{8,16},{16,24},{24,32},{32,40},{40,48},{48,56},{56,6... | collective-permute-start | bytes 442376 | tf_op jit(solution)/shard_map/ppermute | solution.py:16
  167.3 5.3 %collective-permute-done.16 = bf16[128,128]{1,0:T(8,128)(2,1)S(1)} collective-permute-done((bf16[128,128]{1,0:T(8,128)(2,1)}, bf16[128,128]{1,0:T(8,128)(2,1)S(1)}, u32[]{:S(2)}, u32[]{:S(2)}) %collective-permute-start.16) | collective-permute-done | bytes 32800 | tf_op jit(solution)/shard_map/ppermute | solution.py:16
  176.4 4.9 %all-to-all-start.6 = ((f32[8,1,32768]{2,1,0:T(1,128)}), f32[8,1,32768]{2,1,0:T(1,128)}, u32[]{:S(2)}, u32[]{:S(2)}) async-start(f32[8,1,32768]{2,1,0:T(1,128)} %broadcast_in_dim.102), calls=%async_computation.6 | async-start | bytes 2097152 | tf_op jit(solution)/shard_map/all_to_all | solution.py:21
  189.3 6.6 %collective-permute-done.19 = bf16[128,128]{1,0:T(8,128)(2,1)S(1)} collective-permute-done((bf16[128,128]{1,0:T(8,128)(2,1)S(1)}, bf16[128,128]{1,0:T(8,128)(2,1)S(1)}, u32[]{:S(2)}, u32[]{:S(2)}) %collective-permute-start.19) | collective-permute-done | bytes 32800 | tf_op jit(solution)/shard_map/ppermute | solution.py:16
  207.3 5.4 %collective-permute-start = (f32[128,128]{1,0:T(8,128)S(1)}, f32[128,128]{1,0:T(8,128)S(1)}, u32[]{:S(2)}, u32[]{:S(2)}) collective-permute-start(f32[128,128]{1,0:T(8,128)S(1)} %get-tuple-element.854), channel_id=1, source_target_pairs={{504,0},{0,8},{8,16},{16,24},{24,32},{32,40},{40,48},{48,56},{56,6... | collective-permute-start | bytes 196616 | tf_op jit(solution)/shard_map/ppermute | solution.py:16
  215.6 4.4 %collective-permute-start.3 = (f32[128,128]{1,0:T(8,128)S(1)}, f32[128,128]{1,0:T(8,128)S(1)}, u32[]{:S(2)}, u32[]{:S(2)}) collective-permute-start(f32[128,128]{1,0:T(8,128)S(1)} %add.151), channel_id=1, source_target_pairs={{504,0},{0,8},{8,16},{16,24},{24,32},{32,40},{40,48},{48,56},{56,6... | collective-permute-start | bytes 196616 | tf_op jit(solution)/shard_map/ppermute | solution.py:16
  226.9 4.8 %collective-permute-start.9 = (f32[128,128]{1,0:T(8,128)S(1)}, f32[128,128]{1,0:T(8,128)S(1)}, u32[]{:S(2)}, u32[]{:S(2)}) collective-permute-start(f32[128,128]{1,0:T(8,128)S(1)} %add.159), channel_id=1, source_target_pairs={{504,0},{0,8},{8,16},{16,24},{24,32},{32,40},{40,48},{48,56},{56,6... | collective-permute-start | bytes 196616 | tf_op jit(solution)/shard_map/ppermute | solution.py:16
  235.4 5.6 %collective-permute-start.12 = (f32[128,128]{1,0:T(8,128)S(1)}, f32[128,128]{1,0:T(8,128)S(1)}, u32[]{:S(2)}, u32[]{:S(2)}) collective-permute-start(f32[128,128]{1,0:T(8,128)S(1)} %add.163), channel_id=1, source_target_pairs={{504,0},{0,8},{8,16},{16,24},{24,32},{32,40},{40,48},{48,56},{56,6... | collective-permute-start | bytes 196616 | tf_op jit(solution)/shard_map/ppermute | solution.py:16
  242.4 5.2 %collective-permute-start.15 = (f32[128,128]{1,0:T(8,128)S(1)}, f32[128,128]{1,0:T(8,128)S(1)}, u32[]{:S(2)}, u32[]{:S(2)}) collective-permute-start(f32[128,128]{1,0:T(8,128)S(1)} %add.167), channel_id=1, source_target_pairs={{504,0},{0,8},{8,16},{16,24},{24,32},{32,40},{40,48},{48,56},{56,6... | collective-permute-start | bytes 196616 | tf_op jit(solution)/shard_map/ppermute | solution.py:16
  254.5 7.7 %collective-permute-start.21 = (f32[128,128]{1,0:T(8,128)S(1)}, f32[128,128]{1,0:T(8,128)S(1)}, u32[]{:S(2)}, u32[]{:S(2)}) collective-permute-start(f32[128,128]{1,0:T(8,128)S(1)} %add.175), channel_id=1, source_target_pairs={{56,0},{64,8},{72,16},{80,24},{88,32},{96,40},{104,48},{112,56},{1... | collective-permute-start | bytes 196616 | tf_op jit(solution)/shard_map/ppermute | solution.py:16
  262.2 15.7 %collective-permute-done.21 = f32[128,128]{1,0:T(8,128)S(1)} collective-permute-done((f32[128,128]{1,0:T(8,128)S(1)}, f32[128,128]{1,0:T(8,128)S(1)}, u32[]{:S(2)}, u32[]{:S(2)}) %collective-permute-start.21) | collective-permute-done | bytes 65568 | tf_op jit(solution)/shard_map/ppermute | solution.py:16
  277.9 16.7 %all_to_all.53 = f32[8,128,128]{2,1,0:T(8,128)S(1)} all-to-all(f32[8,128,128]{2,1,0:T(8,128)S(1)} %broadcast_in_dim.106), channel_id=1, replica_groups=mesh['seq'=64,'head'=8] {'head'}, dimensions={0} | all-to-all | bytes 1048576 | tf_op jit(solution)/shard_map/all_to_all | solution.py:21
  (171 shorter events, 130.1 us)
Async XLA Ops:
  29.9 23.3 %all-to-all-start = ((f32[8,1,32768]{2,1,0:T(1,128)}), f32[8,1,32768]{2,1,0:T(1,128)}, u32[]{:S(2)}, u32[]{:S(2)}) async-start(f32[8,1,32768]{2,1,0:T(1,128)} %broadcast_in_dim.93), calls=%async_computation | async-start | bytes 2097152 | tf_op jit(solution)/shard_map/all_to_all | solution.py:21
  37.4 13.2 %collective-permute-start.2 = (bf16[128,576]{1,0:T(8,128)(2,1)}, bf16[128,576]{1,0:T(8,128)(2,1)S(1)}, u32[]{:S(2)}, u32[]{:S(2)}) collective-permute-start(bf16[128,576]{1,0:T(8,128)(2,1)} %copy.42), channel_id=1, source_target_pairs={{504,0},{0,8},{8,16},{16,24},{24,32},{32,40},{40,48},{48,56},{56,6... | collective-permute-start | bytes 442376 | tf_op jit(solution)/shard_map/ppermute | solution.py:16
  40.5 10.1 %collective-permute-start.1 = (bf16[128,128]{1,0:T(8,128)(2,1)S(1)}, bf16[128,128]{1,0:T(8,128)(2,1)}, u32[]{:S(2)}, u32[]{:S(2)}) collective-permute-start(bf16[128,128]{1,0:T(8,128)(2,1)S(1)} %copy-done.21), channel_id=1, source_target_pairs={{504,0},{0,8},{8,16},{16,24},{24,32},{32,40},{40,48},{48,56},{56,6... | collective-permute-start | bytes 98312 | tf_op jit(solution)/shard_map/ppermute | solution.py:16
  54.7 22.3 %all-to-all-start.1 = ((f32[8,1,32768]{2,1,0:T(1,128)}), f32[8,1,32768]{2,1,0:T(1,128)}, u32[]{:S(2)}, u32[]{:S(2)}) async-start(f32[8,1,32768]{2,1,0:T(1,128)} %broadcast_in_dim.97), calls=%async_computation.1 | async-start | bytes 2097152 | tf_op jit(solution)/shard_map/all_to_all | solution.py:21
  59.4 15.3 %collective-permute-start.5 = (bf16[128,576]{1,0:T(8,128)(2,1)}, bf16[128,576]{1,0:T(8,128)(2,1)S(1)}, u32[]{:S(2)}, u32[]{:S(2)}) collective-permute-start(bf16[128,576]{1,0:T(8,128)(2,1)} %copy-done.12), channel_id=1, source_target_pairs={{504,0},{0,8},{8,16},{16,24},{24,32},{32,40},{40,48},{48,56},{56,6... | collective-permute-start | bytes 442376 | tf_op jit(solution)/shard_map/ppermute | solution.py:16
  78.5 22.3 %all-to-all-start.2 = ((f32[8,1,32768]{2,1,0:T(1,128)}), f32[8,1,32768]{2,1,0:T(1,128)}, u32[]{:S(2)}, u32[]{:S(2)}) async-start(f32[8,1,32768]{2,1,0:T(1,128)} %broadcast_in_dim.98), calls=%async_computation.2 | async-start | bytes 2097152 | tf_op jit(solution)/shard_map/all_to_all | solution.py:21
  83.4 15.2 %collective-permute-start.8 = (bf16[128,576]{1,0:T(8,128)(2,1)S(1)}, bf16[128,576]{1,0:T(8,128)(2,1)}, u32[]{:S(2)}, u32[]{:S(2)}) collective-permute-start(bf16[128,576]{1,0:T(8,128)(2,1)S(1)} %copy-done.4), channel_id=1, source_target_pairs={{504,0},{0,8},{8,16},{16,24},{24,32},{32,40},{40,48},{48,56},{56,6... | collective-permute-start | bytes 442376 | tf_op jit(solution)/shard_map/ppermute | solution.py:16
  87.3 11.3 %collective-permute-start.7 = (bf16[128,128]{1,0:T(8,128)(2,1)S(1)}, bf16[128,128]{1,0:T(8,128)(2,1)}, u32[]{:S(2)}, u32[]{:S(2)}) collective-permute-start(bf16[128,128]{1,0:T(8,128)(2,1)S(1)} %collective-permute-done.4), channel_id=1, source_target_pairs={{504,0},{0,8},{8,16},{16,24},{24,32},{32,40},{40,48},{48,56},{56,6... | collective-permute-start | bytes 98312 | tf_op jit(solution)/shard_map/ppermute | solution.py:16
  102.4 24.4 %all-to-all-start.3 = ((f32[8,1,32768]{2,1,0:T(1,128)}), f32[8,1,32768]{2,1,0:T(1,128)}, u32[]{:S(2)}, u32[]{:S(2)}) async-start(f32[8,1,32768]{2,1,0:T(1,128)} %broadcast_in_dim.99), calls=%async_computation.3 | async-start | bytes 2097152 | tf_op jit(solution)/shard_map/all_to_all | solution.py:21
  106.6 14.7 %collective-permute-start.11 = (bf16[128,576]{1,0:T(8,128)(2,1)}, bf16[128,576]{1,0:T(8,128)(2,1)S(1)}, u32[]{:S(2)}, u32[]{:S(2)}) collective-permute-start(bf16[128,576]{1,0:T(8,128)(2,1)} %collective-permute-done.8), channel_id=1, source_target_pairs={{504,0},{0,8},{8,16},{16,24},{24,32},{32,40},{40,48},{48,56},{56,6... | collective-permute-start | bytes 442376 | tf_op jit(solution)/shard_map/ppermute | solution.py:16
  110.6 10.7 %collective-permute-start.10 = (bf16[128,128]{1,0:T(8,128)(2,1)}, bf16[128,128]{1,0:T(8,128)(2,1)S(1)}, u32[]{:S(2)}, u32[]{:S(2)}) collective-permute-start(bf16[128,128]{1,0:T(8,128)(2,1)} %collective-permute-done.7), channel_id=1, source_target_pairs={{504,0},{0,8},{8,16},{16,24},{24,32},{32,40},{40,48},{48,56},{56,6... | collective-permute-start | bytes 98312 | tf_op jit(solution)/shard_map/ppermute | solution.py:16
  128.3 23.4 %all-to-all-start.4 = ((f32[8,1,32768]{2,1,0:T(1,128)}), f32[8,1,32768]{2,1,0:T(1,128)}, u32[]{:S(2)}, u32[]{:S(2)}) async-start(f32[8,1,32768]{2,1,0:T(1,128)} %broadcast_in_dim.100), calls=%async_computation.4 | async-start | bytes 2097152 | tf_op jit(solution)/shard_map/all_to_all | solution.py:21
  134.4 14.8 %collective-permute-start.14 = (bf16[128,576]{1,0:T(8,128)(2,1)S(1)}, bf16[128,576]{1,0:T(8,128)(2,1)}, u32[]{:S(2)}, u32[]{:S(2)}) collective-permute-start(bf16[128,576]{1,0:T(8,128)(2,1)S(1)} %copy-done.7), channel_id=1, source_target_pairs={{504,0},{0,8},{8,16},{16,24},{24,32},{32,40},{40,48},{48,56},{56,6... | collective-permute-start | bytes 442376 | tf_op jit(solution)/shard_map/ppermute | solution.py:16
  138.3 10.8 %collective-permute-start.13 = (bf16[128,128]{1,0:T(8,128)(2,1)S(1)}, bf16[128,128]{1,0:T(8,128)(2,1)}, u32[]{:S(2)}, u32[]{:S(2)}) collective-permute-start(bf16[128,128]{1,0:T(8,128)(2,1)S(1)} %collective-permute-done.10), channel_id=1, source_target_pairs={{504,0},{0,8},{8,16},{16,24},{24,32},{32,40},{40,48},{48,56},{56,6... | collective-permute-start | bytes 98312 | tf_op jit(solution)/shard_map/ppermute | solution.py:16
  153.3 21.6 %all-to-all-start.5 = ((f32[8,1,32768]{2,1,0:T(1,128)}), f32[8,1,32768]{2,1,0:T(1,128)}, u32[]{:S(2)}, u32[]{:S(2)}) async-start(f32[8,1,32768]{2,1,0:T(1,128)} %broadcast_in_dim.101), calls=%async_computation.5 | async-start | bytes 2097152 | tf_op jit(solution)/shard_map/all_to_all | solution.py:21
  157.5 15.1 %collective-permute-start.17 = (bf16[128,576]{1,0:T(8,128)(2,1)}, bf16[128,576]{1,0:T(8,128)(2,1)S(1)}, u32[]{:S(2)}, u32[]{:S(2)}) collective-permute-start(bf16[128,576]{1,0:T(8,128)(2,1)} %collective-permute-done.14), channel_id=1, source_target_pairs={{504,0},{0,8},{8,16},{16,24},{24,32},{32,40},{40,48},{48,56},{56,6... | collective-permute-start | bytes 442376 | tf_op jit(solution)/shard_map/ppermute | solution.py:16
  164.8 7.8 %collective-permute-start.16 = (bf16[128,128]{1,0:T(8,128)(2,1)}, bf16[128,128]{1,0:T(8,128)(2,1)S(1)}, u32[]{:S(2)}, u32[]{:S(2)}) collective-permute-start(bf16[128,128]{1,0:T(8,128)(2,1)} %collective-permute-done.13), channel_id=1, source_target_pairs={{504,0},{0,8},{8,16},{16,24},{24,32},{32,40},{40,48},{48,56},{56,6... | collective-permute-start | bytes 98312 | tf_op jit(solution)/shard_map/ppermute | solution.py:16
  176.4 22.4 %all-to-all-start.6 = ((f32[8,1,32768]{2,1,0:T(1,128)}), f32[8,1,32768]{2,1,0:T(1,128)}, u32[]{:S(2)}, u32[]{:S(2)}) async-start(f32[8,1,32768]{2,1,0:T(1,128)} %broadcast_in_dim.102), calls=%async_computation.6 | async-start | bytes 2097152 | tf_op jit(solution)/shard_map/all_to_all | solution.py:21
  181.3 14.6 %collective-permute-start.20 = (bf16[128,576]{1,0:T(8,128)(2,1)S(1)}, bf16[128,576]{1,0:T(8,128)(2,1)}, u32[]{:S(2)}, u32[]{:S(2)}) collective-permute-start(bf16[128,576]{1,0:T(8,128)(2,1)S(1)} %copy-done.10), channel_id=1, source_target_pairs={{504,0},{0,8},{8,16},{16,24},{24,32},{32,40},{40,48},{48,56},{56,6... | collective-permute-start | bytes 442376 | tf_op jit(solution)/shard_map/ppermute | solution.py:16
  185.3 10.6 %collective-permute-start.19 = (bf16[128,128]{1,0:T(8,128)(2,1)S(1)}, bf16[128,128]{1,0:T(8,128)(2,1)S(1)}, u32[]{:S(2)}, u32[]{:S(2)}) collective-permute-start(bf16[128,128]{1,0:T(8,128)(2,1)S(1)} %collective-permute-done.16), channel_id=1, source_target_pairs={{504,0},{0,8},{8,16},{16,24},{24,32},{32,40},{40,48},{48,56},{56,6... | collective-permute-start | bytes 98312 | tf_op jit(solution)/shard_map/ppermute | solution.py:16
  200.3 52.8 %all-to-all-start.7 = ((f32[8,1,32768]{2,1,0:T(1,128)}), f32[8,1,32768]{2,1,0:T(1,128)S(1)}, u32[]{:S(2)}, u32[]{:S(2)}) async-start(f32[8,1,32768]{2,1,0:T(1,128)} %broadcast_in_dim.105), calls=%async_computation.7 | async-start | bytes 2097152 | tf_op jit(solution)/shard_map/all_to_all | solution.py:21
  207.3 8.3 %collective-permute-start = (f32[128,128]{1,0:T(8,128)S(1)}, f32[128,128]{1,0:T(8,128)S(1)}, u32[]{:S(2)}, u32[]{:S(2)}) collective-permute-start(f32[128,128]{1,0:T(8,128)S(1)} %get-tuple-element.854), channel_id=1, source_target_pairs={{504,0},{0,8},{8,16},{16,24},{24,32},{32,40},{40,48},{48,56},{56,6... | collective-permute-start | bytes 196616 | tf_op jit(solution)/shard_map/ppermute | solution.py:16
  226.9 8.5 %collective-permute-start.9 = (f32[128,128]{1,0:T(8,128)S(1)}, f32[128,128]{1,0:T(8,128)S(1)}, u32[]{:S(2)}, u32[]{:S(2)}) collective-permute-start(f32[128,128]{1,0:T(8,128)S(1)} %add.159), channel_id=1, source_target_pairs={{504,0},{0,8},{8,16},{16,24},{24,32},{32,40},{40,48},{48,56},{56,6... | collective-permute-start | bytes 196616 | tf_op jit(solution)/shard_map/ppermute | solution.py:16
  254.5 23.5 %collective-permute-start.21 = (f32[128,128]{1,0:T(8,128)S(1)}, f32[128,128]{1,0:T(8,128)S(1)}, u32[]{:S(2)}, u32[]{:S(2)}) collective-permute-start(f32[128,128]{1,0:T(8,128)S(1)} %add.175), channel_id=1, source_target_pairs={{56,0},{64,8},{72,16},{80,24},{88,32},{96,40},{104,48},{112,56},{1... | collective-permute-start | bytes 196616 | tf_op jit(solution)/shard_map/ppermute | solution.py:16
  (25 other events, 210.2 us)
where the time goes:
time: 296 us; the launch traced here: 295 us
  starting transfers between devices  131 us (44%)
  waiting for transfers between devices  81.2 us (27%)
  local copies, waits for them, and re-layouts  26.2 us (9%)
  blocking collectives  16.7 us (6%)
  between operations  16.5 us (6%)
  other arithmetic  15.3 us (5%)
  matrix products  8.24 us (3%)
    ppermute x22, starting transfers between devices, passed_along(): return lax.ppermute(block, axis, route)  90.9 us
    ppermute x22, waiting for transfers between devices, passed_along(): return lax.ppermute(block, axis, route)  73.8 us
    all_to_all x8, starting transfers between devices, copy_for_each(): lax.all_to_all(jnp.broadcast_to(value[None], (length, *value.shape)), axi...  39.8 us
    all_to_all x1, blocking collectives, copy_for_each(): lax.all_to_all(jnp.broadcast_to(value[None], (length, *value.shape)), axi...  16.7 us
    broadcast_in_dim x9, local copies, waits for them, and re-layouts, copy_for_each(): jnp.broadcast_to(value[None], (length, *value.shape))  12.3 us
    unnamed x38, local copies, waits for them, and re-layouts  7.45 us
    all_to_all x8, waiting for transfers between devices, copy_for_each(): lax.all_to_all(jnp.broadcast_to(value[None], (length, *value.shape)), axi...  7.41 us
    reduce_sum x2, other arithmetic, pick_entry(): return jnp.sum(jnp.where(positions == wanted, table, 0))  7.19 us
  transfers between devices with their start and end apart: 30, of which 20 were waited for; matrix products, arithmetic and copies ran while one was open for 6% of the time, Pallas kernels for 0%

commit v1 on v0

v1 whole, which is shorter than its diff:
```python
import math

import jax
import jax.numpy as jnp
from jax import lax
from jax.experimental import pallas as pl
from jax.experimental.pallas import tpu as pltpu
from jax.sharding import PartitionSpec as P

HEADS = 128
HOPS = 8
NX = 4

MESH = pl.DeviceIdType.MESH
F32 = jnp.float32
BF16 = jnp.bfloat16
MAIN_SCALE = 1.0 / 192.0**0.5
LOG2E = math.log2(math.e)
NT = (((1,), (1,)), ((), ()))


def dot_nt(a, b):
    return lax.dot_general(a, b, NT, preferred_element_type=F32)


def make_kernel(nseq, nh):
    T = 128
    TS = T // nh
    HL = 128 // nh
    JL = 64 // nh
    PR = nh - 1
    HALF, QUART = T // 2, T // 4
    index_scale = 1.0 / 128.0**0.5
    UNROLL = 4
    SLOTS = ((0, 1), (1, 2), (3, 2), (5, 2), (7, 1))

    def kernel(
        q_hbm, lat_hbm, lse_hbm, iq_hbm, iw_hbm, ik_hbm, lsei_hbm, order_hbm, blive_hbm,
        out_ref,
        q, lat_t, kl, ki, lse, iq, iqt, iw, wb, lsei, order, blive, mask, mt,
        m0, m1, m2, m3, m4, r0, r1, r2, r3, r4,
        x0, x1, x2, x3, x4, lg0, lg1, lg2, lg3, lg4, wt,
        g0, g1, g2, g3, g4, h0, h1, h2, h3, h4,
        o0, o1, o2, o3, o4, orecv, fin,
        loc, zs, zr, xs, xr, ds, dr, iqs, iqr, ws, wr, ms, mr, gs, gr, osem, orsem, as_, ar,
    ):
        M = (m0, m1, m2, m3, m4)
        RM = (r0, r1, r2, r3, r4)
        X = (x0, x1, x2, x3, x4)
        LG = (lg0, lg1, lg2, lg3, lg4)
        G = (g0, g1, g2, g3, g4)
        RG = (h0, h1, h2, h3, h4)
        O = (o0, o1, o2, o3, o4)
        d = lax.axis_index("seq")
        h = lax.axis_index("head")
        c = lax.rem(d, 2)
        x = lax.rem(h, NX)
        yh = h - x
        half = pl.multiple_of(HALF * lax.rem(x, 2), HALF)
        quart = pl.multiple_of(half + QUART * (x // 2), QUART)

        def seq(offset):
            return lax.rem(d + offset + nseq, nseq)

        def peer(r):
            return lax.rem(h + r, nh)

        def xpeer(step):
            return yh + lax.rem(x + step, NX)

        barrier = pltpu.get_barrier_semaphore()
        for r in range(1, nh):
            pl.semaphore_signal(barrier, inc=1, device_id=(d, peer(r)), device_id_type=MESH)
        for k in range(1, HOPS):
            pl.semaphore_signal(barrier, inc=1, device_id=(seq(k), h), device_id_type=MESH)
            pl.semaphore_signal(barrier, inc=1, device_id=(seq(-k), h), device_id_type=MESH)

        mine = pl.ds(pl.multiple_of(h * TS, TS), TS)
        my_rows = pl.ds(pl.multiple_of(h * TS * JL, TS * JL), TS * JL)
        locals_ = [
            pltpu.make_async_copy(lat_hbm, lat_t, loc.at[0]),
            pltpu.make_async_copy(q_hbm, q, loc.at[1]),
            pltpu.make_async_copy(lse_hbm, lse, loc.at[2]),
            pltpu.make_async_copy(ik_hbm, ki.at[0], loc.at[3]),
            pltpu.make_async_copy(iq_hbm.at[my_rows, :], iq.at[PR], loc.at[4]),
            pltpu.make_async_copy(iw_hbm, iw.at[PR], loc.at[5]),
            pltpu.make_async_copy(lsei_hbm, lsei, loc.at[6]),
            pltpu.make_async_copy(order_hbm, order, loc.at[7]),
            pltpu.make_async_copy(blive_hbm, blive, loc.at[8]),
        ]
        for cp in locals_:
            cp.start()
        for cp in locals_:
            cp.wait()

        kl[0] = lat_t[...].T
        lse[...] = lse[...] * LOG2E

        pl.semaphore_wait(barrier, PR + 2 * (HOPS - 1))

        def rcopy(src, dst, s, r, dev):
            return pltpu.make_async_remote_copy(
                src_ref=src, dst_ref=dst, send_sem=s, recv_sem=r, device_id=dev, device_id_type=MESH
            )

        def pieces(src_l, src_i, block, rows, s, r, dev):
            return [
                rcopy(src_l.at[rows, :], kl.at[block, rows, :], s.at[0], r.at[0], dev),
                rcopy(src_i.at[rows, :], ki.at[block, rows, :], s.at[1], r.at[1], dev),
            ]

        def kpieces(block, rows, s, r, dev):
            return pieces(kl.at[block], ki.at[block], block, rows, s, r, dev)

        halfrows = pl.ds(half, HALF)
        quartrows = pl.ds(quart, QUART)
        allrows = pl.ds(0, T)

        def zcopies(j):
            if j < 4:
                return pieces(kl.at[0], ki.at[0], 2 * j - 1 + c, halfrows, zs.at[j - 1], zr.at[j - 1], (seq(2 * j), h))
            return pieces(kl.at[0], ki.at[0], 7, halfrows, zs.at[3], zr.at[3], (seq(7), h))

        def own_to_partner():
            return pieces(kl.at[0], ki.at[0], 7, allrows, ds.at[3], dr.at[3], (seq(1), h))

        for cp in zcopies(1):
            cp.start()
        for r in range(1, nh):
            to = peer(r)
            rows = pl.ds(pl.multiple_of(to * TS * JL, TS * JL), TS * JL)
            rcopy(iq_hbm.at[rows, :], iq.at[r - 1], iqs, iqr, (d, to)).start()
            rcopy(iw_hbm, iw.at[r - 1], ws, wr, (d, to)).start()
        for j in (2, 3):
            for cp in zcopies(j):
                cp.start()

        @pl.when(c == 1)
        def _():
            for cp in zcopies(4):
                cp.start()

        @pl.when(c == 0)
        def _():
            for cp in own_to_partner():
                cp.start()

        lane64 = lax.broadcasted_iota(jnp.int32, (1, nseq), 1)
        order_f = order[...].astype(F32)

        def entry(at):
            return jnp.sum(jnp.where(lane64 == at, order_f, 0.0), axis=1, keepdims=True)

        own_slab = entry(d)
        row64 = lax.broadcasted_iota(jnp.int32, (nseq, nseq), 0).astype(F32)
        live_row = jnp.sum(jnp.where(row64 == own_slab, blive[...].astype(F32), 0.0), axis=0, keepdims=True)
        lane64f = lane64.astype(F32)
        t_at = (h * TS + lax.broadcasted_iota(jnp.int32, (TS, T), 0)).astype(F32) + own_slab * T
        s_in = lax.broadcasted_iota(jnp.int32, (TS, T), 1).astype(F32)
        hops = [0 * c] + [2 * j + c - cc for j in (1, 2, 3) for cc in (0, 1)] + [7 - 6 * c]
        for b in range(8):
            slab = entry(seq(-hops[b]))
            allowed = jnp.sum(jnp.where(lane64f == slab, live_row, 0.0), axis=1, keepdims=True)
            mask[b] = jnp.where((s_in + slab * T <= t_at) & (allowed == 1.0), 1.0, 0.0)
        lane_t = lax.broadcasted_iota(jnp.int32, (TS, T), 1)
        row_t = h * TS + lax.broadcasted_iota(jnp.int32, (TS, T), 0)
        lse_col = jnp.sum(jnp.where(lane_t == row_t, lsei[...], 0.0), axis=1, keepdims=True)

        def mass(si):
            b0, nb = SLOTS[si]
            rows = pl.ds(0, nb * T)
            mt[rows, :] = jnp.zeros((nb * T, T), F32)

            @pl.loop(0, HL // (2 * UNROLL))
            def _(i):
                keys = kl[b0 : b0 + nb].reshape(nb * T, 576)
                part = None
                for u in range(UNROLL):
                    h0 = 2 * (i * UNROLL + u)
                    sc = jnp.dot(keys, jnp.concatenate([q[h0], q[h0 + 1]], axis=1), preferred_element_type=F32)
                    for v in range(2):
                        e = jnp.exp2(sc[:, v * T : (v + 1) * T] * (MAIN_SCALE * LOG2E) - lse[pl.ds(h0 + v, 1), :])
                        part = e if part is None else part + e
                mt[rows, :] += part

            for b in range(nb):
                M[si][:, b * T : (b + 1) * T] = mt[b * T : (b + 1) * T, :].T

            for r in range(1, nh):
                to = peer(r)
                toks = pl.ds(pl.multiple_of(to * TS, TS), TS)
                rcopy(M[si].at[toks, :], RM[si].at[r - 1], ms.at[si], mr.at[si], (d, to)).start()

        def wait_all(ref, sem):
            pltpu.make_async_copy(ref, ref, sem).wait()

        def wait_recv(copies):
            for cp in copies:
                cp.wait_recv()

        def z_arrived(j):
            wait_recv(kpieces(2 * j - 1 + c if j < 4 else 7, halfrows, zs.at[j - 1], zr.at[j - 1], (d, h)))

        def x_copies(j, way):
            return kpieces(2 * j - 1 + c if j < 4 else 7, quartrows, xs.at[j - 1, way], xr.at[j - 1, way], (d, xpeer((1, NX - 1)[way])))

        def x_forward(j):
            for way in (0, 1):
                for cp in x_copies(j, way):
                    cp.start()

        def x_arrived(j):
            for way in (0, 1):
                wait_recv(x_copies(j, way))

        def d_copies(j):
            return kpieces(2 * j - 1 + c, allrows, ds.at[j - 1], dr.at[j - 1], (d + 1 - 2 * c, h))

        def d_forward(j):
            for cp in d_copies(j):
                cp.start()

        def relay_z(j):
            z_arrived(j)
            x_forward(j)

        def relay_x(j):
            x_arrived(j)
            d_forward(j)

        def index_tables():
            wait_all(iq.at[0:PR], iqr)
            wait_all(iw.at[0:PR], wr)
            eye = jnp.where(
                lax.broadcasted_iota(jnp.int32, (T, T), 0) == lax.broadcasted_iota(jnp.int32, (T, T), 1), 1.0, 0.0
            ).astype(BF16)
            pick = lax.broadcasted_iota(jnp.int32, (TS, JL, T), 0) + h * TS == lax.broadcasted_iota(jnp.int32, (TS, JL, T), 2)
            for hh in range(nh):
                iqt[:, hh * T : (hh + 1) * T] = dot_nt(eye, iq[hh]).astype(BF16)
                w = jnp.broadcast_to(iw[hh][None], (TS, JL, T))
                col = jnp.sum(jnp.where(pick, w, 0.0), axis=2, keepdims=True).reshape(TS * JL, 1)
                wb[hh] = jnp.broadcast_to(col, (TS * JL, T))

        def wide(v, nb):
            return jnp.concatenate([v] * nb, axis=1) if nb > 1 else v

        def phase_a(si):
            b0, nb = SLOTS[si]
            keys = ki[b0 : b0 + nb].reshape(nb * T, T)
            LG[si][...] = jnp.zeros_like(LG[si])

            @pl.loop(0, nh)
            def _(hh):
                xv = dot_nt(iq[hh], keys)
                X[si][hh] = xv
                LG[si][...] += jnp.sum(
                    (jnp.maximum(xv, 0.0) * wide(wb[hh], nb)).reshape(TS, JL, nb * T), axis=1
                )

        def phase_b(si):
            b0, nb = SLOTS[si]
            wait_all(RM[si], mr.at[si])
            total = M[si][mine, :]
            for r in range(PR):
                total = total + RM[si][r]
            live = jnp.concatenate([mask[b0 + b] for b in range(nb)], axis=1) if nb > 1 else mask[b0]
            g = jnp.where(live > 0.0, jnp.exp(LG[si][...] * index_scale - lse_col) - total * (1.0 / HEADS), 0.0)
            LG[si][...] = g

            @pl.loop(0, nh)
            def _(hh):
                rows = pl.ds(pl.multiple_of(hh * TS * JL, TS * JL), TS * JL)
                gv = jnp.broadcast_to(LG[si][...][:, None, :], (TS, JL, nb * T)).reshape(TS * JL, nb * T)
                wt[rows, 0 : nb * T] = jnp.where(X[si][hh] > 0.0, gv * wide(wb[hh], nb), 0.0).astype(BF16)

            G[si][...] = jnp.dot(iqt[...], wt[:, 0 : nb * T], preferred_element_type=F32)
            for r in range(1, nh):
                to = peer(r)
                toks = pl.ds(pl.multiple_of(to * TS, TS), TS)
                rcopy(G[si].at[toks, :], RG[si].at[r - 1], gs.at[si], gr.at[si], (d, to)).start()

        def phase_c(si):
            b0, nb = SLOTS[si]
            wait_all(RG[si], gr.at[si])
            total = G[si][mine, :]
            for r in range(PR):
                total = total + RG[si][r]
            O[si][...] = total
            if si > 0:
                for b in range(nb):
                    k = hops[b0 + b]
                    rcopy(
                        O[si].at[:, b * T : (b + 1) * T], orecv.at[k - 1], osem, orsem, (seq(-k), h)
                    ).start()

        mass(0)
        relay_z(1)
        relay_z(2)
        relay_x(1)
        relay_z(3)
        index_tables()
        phase_a(0)
        wait_d = lambda j: wait_recv(
            kpieces(2 * j - c, allrows, ds.at[j - 1], dr.at[j - 1], (d, h))
        )
        wait_d(1)
        mass(1)
        phase_a(1)
        relay_x(2)

        @pl.when(c == 0)
        def _():
            relay_z(4)

        wait_d(2)
        mass(2)
        phase_a(2)
        phase_b(0)
        relay_x(3)
        wait_d(3)
        mass(3)
        phase_a(3)
        phase_b(1)

        @pl.when(c == 0)
        def _():
            x_arrived(4)

        @pl.when(c == 1)
        def _():
            wait_recv(own_to_partner())

        mass(4)
        phase_a(4)
        phase_c(0)
        phase_b(2)
        phase_c(1)
        phase_b(3)
        phase_c(2)
        phase_b(4)
        phase_c(3)
        phase_c(4)

        wait_all(orecv, orsem)
        total = O[0][...]
        for k in range(HOPS - 1):
            total = total + orecv[k]
        fin[mine, :] = total * index_scale
        for r in range(1, nh):
            rcopy(fin.at[mine, :], fin.at[mine, :], as_, ar, (d, peer(r))).start()
        wait_all(orecv, ar) if TS * PR * T == (HOPS - 1) * TS * T else None
        out_ref[...] = fin[...].T

        for j in (1, 2, 3):
            for cp in zcopies(j) + x_copies(j, 0) + x_copies(j, 1) + d_copies(j):
                cp.wait_send()

        @pl.when(c == 1)
        def _():
            for cp in zcopies(4):
                cp.wait_send()

        @pl.when(c == 0)
        def _():
            for cp in own_to_partner() + x_copies(4, 0) + x_copies(4, 1):
                cp.wait_send()

        wait_all(iq.at[0:PR], iqs)
        wait_all(iw.at[0:PR], ws)
        for si in range(5):
            wait_all(RM[si], ms.at[si])
            wait_all(RG[si], gs.at[si])
        wait_all(orecv, osem)
        wait_all(orecv, as_)

    def slots(make):
        return [make(nb) for _, nb in SLOTS]

    dma = pltpu.SemaphoreType.DMA
    scratch = [
        pltpu.VMEM((HL, 576, T), BF16),
        pltpu.VMEM((576, T), BF16),
        pltpu.VMEM((8, T, 576), BF16),
        pltpu.VMEM((8, T, T), BF16),
        pltpu.VMEM((HL, T), F32),
        pltpu.VMEM((nh, TS * JL, T), BF16),
        pltpu.VMEM((T, nh * TS * JL), BF16),
        pltpu.VMEM((nh, JL, T), F32),
        pltpu.VMEM((nh, TS * JL, T), F32),
        pltpu.VMEM((1, T), F32),
        pltpu.VMEM((1, nseq), jnp.int32),
        pltpu.VMEM((nseq, nseq), jnp.int32),
        pltpu.VMEM((8, TS, T), F32),
        pltpu.VMEM((2 * T, T), F32),
        *slots(lambda nb: pltpu.VMEM((T, nb * T), F32)),
        *slots(lambda nb: pltpu.VMEM((PR, TS, nb * T), F32)),
        *slots(lambda nb: pltpu.VMEM((nh, TS * JL, nb * T), F32)),
        *slots(lambda nb: pltpu.VMEM((TS, nb * T), F32)),
        pltpu.VMEM((nh * TS * JL, 2 * T), BF16),
        *slots(lambda nb: pltpu.VMEM((T, nb * T), F32)),
        *slots(lambda nb: pltpu.VMEM((PR, TS, nb * T), F32)),
        *slots(lambda nb: pltpu.VMEM((TS, nb * T), F32)),
        pltpu.VMEM((HOPS - 1, TS, T), F32),
        pltpu.VMEM((T, T), F32),
        dma((9,)), dma((4, 2)), dma((4, 2)), dma((4, 2, 2)), dma((4, 2, 2)), dma((4, 2)), dma((4, 2)),
        dma, dma, dma, dma, dma((5,)), dma((5,)), dma((5,)), dma((5,)), dma, dma, dma, dma,
    ]
    return kernel, scratch


def solution(mesh):
    nseq, nh = mesh.shape["seq"], mesh.shape["head"]
    kernel, scratch = make_kernel(nseq, nh)

    def local(q_main, latent_keys, lse_main, index_queries, index_weights, index_keys, lse_index, slab_order, block_live):
        return pl.pallas_call(
            kernel,
            out_shape=jax.ShapeDtypeStruct(index_keys.shape, F32),
            in_specs=[pl.BlockSpec(memory_space=pltpu.HBM)] * 9,
            out_specs=pl.BlockSpec(memory_space=pltpu.VMEM),
            scratch_shapes=scratch,
            compiler_params=pltpu.CompilerParams(
                collective_id=0, has_side_effects=True, vmem_limit_bytes=60 * 2**20
            ),
        )(
            q_main.transpose(1, 2, 0),
            latent_keys.T,
            lse_main.T,
            index_queries.reshape(-1, index_queries.shape[2]),
            index_weights.T,
            index_keys,
            lse_index.reshape(1, -1),
            slab_order.reshape(1, -1),
            block_live,
        )

    placed = (
        P("seq", "head", None), P("seq", None), P("seq", "head"), P("seq", "head", None), P("seq", "head"),
        P("seq", None), P("seq"), P(), P(),
    )
    return jax.shard_map(local, mesh=mesh, in_specs=placed, out_specs=P("seq", None), check_vma=False)
```

time: 296 us -> 64.3 us (0.22)
  the two profiles are of different devices: /device:TPU:65 before, /device:TPU:1 now
where the time goes in v1:
time: 64.3 us; the launch traced here: 64.1 us
  Pallas kernels  62.7 us (98%)
  local copies, waits for them, and re-layouts  1.47 us (2%)
    pallas_call x1, Pallas kernels, local(): pl.pallas_call(kernel, out_shape=jax.ShapeDtypeStruct(index_keys.shape, F...  62.7 us
    unnamed x1, local copies, waits for them, and re-layouts  1.47 us

profile of v1, /device:TPU:1, one launch (start us, length us, event | category | flops | bytes accessed | tf_op | source)
XLA Modules:
  0.0 64.1 jit_solution(8864840221055701448)
XLA Ops:
  0.0 62.7 %shard_map.91 = f32[128,128]{1,0:T(8,128)} custom-call(bf16[16,576,128]{2,1,0:T(8,128)(2,1)} %bitcast.7, bf16[576,128]{1,0:T(8,128)(2,1)} %bitcast.9, f32[16,128]{1,0:T(8,128)} %bitcast.10, bf16[1024,128]{1,0:T(8,128)(2,1)} %bitcast.8, f32[8,128]{1,0:T(8,128)} %bitcast.11, bf16[128,128]{1,0:T(8,128)(2,1)} %ik_hbm.1, f32[1,128]{1,0:T(1,128)} %bitcast.12, ...), custom_call_target="tpu_custom_call" | custom-call | tf_op jit(solution)/shard_map/pallas_call | solution.py:416
  62.7 1.5 %copy.11 = f32[128,128]{1,0:T(8,128)} copy(f32[128,128]{1,0:T(8,128)} %shard_map.91) | data formatting | bytes 131072

commit v2 on v1

v2 whole, which is shorter than its diff:
```python
import math

import jax
import jax.numpy as jnp
from jax import lax
from jax.experimental import pallas as pl
from jax.experimental.pallas import tpu as pltpu
from jax.sharding import PartitionSpec as P

HEADS = 128
HOPS = 8
NX = 4

MESH = pl.DeviceIdType.MESH
F32 = jnp.float32
BF16 = jnp.bfloat16
BIG = 3.0e38
MAIN_SCALE = 1.0 / 192.0**0.5
LOG2E = math.log2(math.e)
NT = (((1,), (1,)), ((), ()))


def dot_nt(a, b):
    return lax.dot_general(a, b, NT, preferred_element_type=F32)


def make_kernel(nseq, nh):
    T = 128
    TS = T // nh
    HL = 128 // nh
    JL = 64 // nh
    PR = nh - 1
    C = 576
    HALF, QUART = (C // 2, T // 2), (C // 4, T // 4)
    index_scale = 1.0 / 128.0**0.5
    GH = 4
    FAR_FIRST = sorted(range(1, nh), key=lambda r: -2 * (r // NX) - min(r % NX, NX - r % NX))
    SLOTS = ((0, 1), (1, 2), (3, 2), (5, 2), (7, 1))

    def kernel(
        q_hbm, lat_hbm, lse_hbm, iq_hbm, iw_hbm, ik_hbm, lsei_hbm, order_hbm, blive_hbm,
        out_ref,
        q, qt, kl, ki, lse, iq, iqt, iw, wb, lsei, order, blive, mask, acc,
        m0, m1, m2, m3, m4, r0, r1, r2, r3, r4,
        x0, x1, x2, x3, x4, lg0, lg1, lg2, lg3, lg4, wt,
        g0, g1, g2, g3, g4, h0, h1, h2, h3, h4,
        o0, o1, o2, o3, o4, orecv, fin,
        mb0, mb1, mb2, mb3, mb4, gb0, gb1, gb2, gb3, gb4,
        loc, zs, zr, xs, xr, ds, dr, iqs, iqr, ws, wr, ms, mr, gs, gr, osem, orsem, as_, ar,
    ):
        M = (m0, m1, m2, m3, m4)
        RM = (r0, r1, r2, r3, r4)
        MB = (mb0, mb1, mb2, mb3, mb4)
        GB = (gb0, gb1, gb2, gb3, gb4)
        X = (x0, x1, x2, x3, x4)
        LG = (lg0, lg1, lg2, lg3, lg4)
        G = (g0, g1, g2, g3, g4)
        RG = (h0, h1, h2, h3, h4)
        O = (o0, o1, o2, o3, o4)
        d = lax.axis_index("seq")
        h = lax.axis_index("head")
        c = lax.rem(d, 2)
        x = lax.rem(h, NX)
        yh = h - x
        odd, high = lax.rem(x, 2), x // 2

        def seq(offset):
            return lax.rem(d + offset + nseq, nseq)

        def peer(r):
            return lax.rem(yh + r // NX * NX, nh) + lax.rem(x + r % NX, NX)

        def xpeer(step):
            return yh + lax.rem(x + step, NX)

        barrier = pltpu.get_barrier_semaphore()
        for r in range(1, nh):
            pl.semaphore_signal(barrier, inc=1, device_id=(d, peer(r)), device_id_type=MESH)
        for k in range(1, HOPS):
            pl.semaphore_signal(barrier, inc=1, device_id=(seq(k), h), device_id_type=MESH)
            pl.semaphore_signal(barrier, inc=1, device_id=(seq(-k), h), device_id_type=MESH)

        mine = pl.ds(pl.multiple_of(h * TS, TS), TS)
        my_rows = pl.ds(pl.multiple_of(h * TS * JL, TS * JL), TS * JL)
        locals_ = [
            pltpu.make_async_copy(lat_hbm, kl.at[0], loc.at[0]),
            pltpu.make_async_copy(q_hbm, q, loc.at[1]),
            pltpu.make_async_copy(lse_hbm, lse, loc.at[2]),
            pltpu.make_async_copy(ik_hbm, ki.at[0], loc.at[3]),
            pltpu.make_async_copy(iq_hbm.at[my_rows, :], iq.at[PR], loc.at[4]),
            pltpu.make_async_copy(iw_hbm, iw.at[PR], loc.at[5]),
            pltpu.make_async_copy(lsei_hbm, lsei, loc.at[6]),
            pltpu.make_async_copy(order_hbm, order, loc.at[7]),
            pltpu.make_async_copy(blive_hbm, blive, loc.at[8]),
        ]
        for cp in locals_:
            cp.start()
        pl.semaphore_wait(barrier, PR + 2 * (HOPS - 1))

        def rcopy(src, dst, s, r, dev):
            return pltpu.make_async_remote_copy(
                src_ref=src, dst_ref=dst, send_sem=s, recv_sem=r, device_id=dev, device_id_type=MESH
            )

        def half_at(i, which):
            return pl.ds(pl.multiple_of(HALF[i] * which, HALF[i]), HALF[i])

        own_half = [half_at(i, odd) for i in range(2)]
        other_half = [half_at(i, 1 - odd) for i in range(2)]
        own_quart = [pl.ds(pl.multiple_of(HALF[i] * odd + QUART[i] * high, QUART[i]), QUART[i]) for i in range(2)]
        whole = [pl.ds(0, C), pl.ds(0, T)]
        keys_at = (kl, ki)

        def pieces(src, block, rows, s, r, dev):
            return [
                rcopy(src[i].at[rows[i], :], keys_at[i].at[block, rows[i], :], s.at[i], r.at[i], dev)
                for i in range(2)
            ]

        def kpieces(block, rows, s, r, dev):
            return pieces((kl.at[block], ki.at[block]), block, rows, s, r, dev)

        own_keys = (lat_hbm, ik_hbm)

        def zcopies(j):
            if j < 4:
                return pieces(own_keys, 2 * j - 1 + c, own_half, zs.at[j - 1], zr.at[j - 1], (seq(2 * j), h))
            return pieces(own_keys, 7, own_half, zs.at[3], zr.at[3], (seq(7), h))

        def own_to_partner():
            return pieces(own_keys, 7, whole, ds.at[3, 0], dr.at[3, 0], (seq(1), h))

        def send_index(rs):
            for r in rs:
                to = peer(r)
                rows = pl.ds(pl.multiple_of(to * TS * JL, TS * JL), TS * JL)
                rcopy(iq_hbm.at[rows, :], iq.at[r - 1], iqs, iqr, (d, to)).start()
                rcopy(iw_hbm, iw.at[r - 1], ws, wr, (d, to)).start()

        def far_sends():
            for cp in zcopies(3):
                cp.start()

            @pl.when(c == 1)
            def _():
                for cp in zcopies(4):
                    cp.start()

            @pl.when(c == 0)
            def _():
                for cp in own_to_partner():
                    cp.start()

        send_index(range(1, NX))
        for j in (1, 2):
            for cp in zcopies(j):
                cp.start()

        for cp in locals_:
            cp.wait()

        @pl.loop(0, HL // 4)
        def _(i):
            for u in range(4):
                a = i * 4 + u
                v = lse[pl.ds(a, 1), :] * (-1.0 / MAIN_SCALE)
                hi = v.astype(BF16).astype(F32)
                mid = (v - hi).astype(BF16).astype(F32)
                low = v - hi - mid
                row = lax.broadcasted_iota(jnp.int32, (64, T), 0)
                ext = jnp.where(row == 0, hi, jnp.where(row == 1, mid, jnp.where(row == 2, low, 0.0)))
                qt[a] = jnp.concatenate([q[a], ext.astype(BF16)], axis=0).T

        far_sends()

        lane64 = lax.broadcasted_iota(jnp.int32, (1, nseq), 1)
        order_f = order[...].astype(F32)

        def entry(at):
            return jnp.sum(jnp.where(lane64 == at, order_f, 0.0), axis=1, keepdims=True)

        own_slab = entry(d)
        row64 = lax.broadcasted_iota(jnp.int32, (nseq, nseq), 0).astype(F32)
        live_row = jnp.sum(jnp.where(row64 == own_slab, blive[...].astype(F32), 0.0), axis=0, keepdims=True)
        lane64f = lane64.astype(F32)
        t_at = (h * TS + lax.broadcasted_iota(jnp.int32, (TS, T), 0)).astype(F32) + own_slab * T
        s_in = lax.broadcasted_iota(jnp.int32, (TS, T), 1).astype(F32)
        hops = [0 * c] + [2 * j + c - cc for j in (1, 2, 3) for cc in (0, 1)] + [7 - 6 * c]
        for b in range(8):
            slab = entry(seq(-hops[b]))
            allowed = jnp.sum(jnp.where(lane64f == slab, live_row, 0.0), axis=1, keepdims=True)
            mask[b] = jnp.where((s_in + slab * T <= t_at) & (allowed == 1.0), 1.0, 0.0)
        lane_t = lax.broadcasted_iota(jnp.int32, (TS, T), 1)
        row_t = h * TS + lax.broadcasted_iota(jnp.int32, (TS, T), 0)
        lse_col = jnp.sum(jnp.where(lane_t == row_t, lsei[...], 0.0), axis=1, keepdims=True)

        def side_by_side(vs):
            return jnp.concatenate(vs, axis=1) if len(vs) > 1 else vs[0]

        def mass(si):
            b0, nb = SLOTS[si]
            ones = jnp.where(lax.broadcasted_iota(jnp.int32, (64, nb * T), 0) < 3, 1.0, 0.0).astype(BF16)
            keys = jnp.concatenate([side_by_side([kl[b0 + b] for b in range(nb)]), ones], axis=0)
            part = None
            for u in range(HL // GH):
                heads = qt[u * GH : (u + 1) * GH].reshape(GH * T, C + 64)
                e = jnp.exp2(jnp.dot(heads, keys, preferred_element_type=F32) * (MAIN_SCALE * LOG2E))
                for v in range(GH):
                    ev = e[v * T : (v + 1) * T]
                    part = ev if part is None else part + ev
            M[si][...] = part
            MB[si][...] = M[si][...].astype(BF16)
            for r in FAR_FIRST:
                to = peer(r)
                toks = pl.ds(pl.multiple_of(to * TS, TS), TS)
                rcopy(MB[si].at[toks, :], RM[si].at[r - 1], ms.at[si], mr.at[si], (d, to)).start()

        def wait_all(ref, sem):
            pltpu.make_async_copy(ref, ref, sem).wait()

        def wait_recv(copies):
            for cp in copies:
                cp.wait_recv()

        def block_of(j):
            return 2 * j - 1 + c if j < 4 else 7

        def x_copies(j, way):
            return kpieces(
                block_of(j), own_quart, xs.at[j - 1, way], xr.at[j - 1, way], (d, xpeer((1, NX - 1)[way]))
            )

        def d_copies(j, part):
            rows = (own_half, other_half)[part]
            return kpieces(2 * j - 1 + c, rows, ds.at[j - 1, part], dr.at[j - 1, part], (d + 1 - 2 * c, h))

        def relay_z(j):
            wait_recv(kpieces(block_of(j), own_half, zs.at[j - 1], zr.at[j - 1], (d, h)))
            for way in (0, 1):
                for cp in x_copies(j, way):
                    cp.start()
            if j < 4:
                for cp in d_copies(j, 0):
                    cp.start()

        def x_arrived(j):
            for way in (0, 1):
                wait_recv(x_copies(j, way))

        def relay_x(j):
            x_arrived(j)
            for cp in d_copies(j, 1):
                cp.start()

        def wait_d(j):
            for part in (0, 1):
                rows = (own_half, other_half)[part]
                wait_recv(kpieces(2 * j - c, rows, ds.at[j - 1, part], dr.at[j - 1, part], (d, h)))

        def index_tables():
            wait_all(iq.at[0:PR], iqr)
            wait_all(iw.at[0:PR], wr)
            eye = jnp.where(
                lax.broadcasted_iota(jnp.int32, (T, T), 0) == lax.broadcasted_iota(jnp.int32, (T, T), 1), 1.0, 0.0
            ).astype(BF16)
            pick = lax.broadcasted_iota(jnp.int32, (TS, JL, T), 0) + h * TS == lax.broadcasted_iota(jnp.int32, (TS, JL, T), 2)
            for hh in range(nh):
                iqt[:, hh * T : (hh + 1) * T] = dot_nt(eye, iq[hh]).astype(BF16)
                w = jnp.broadcast_to(iw[hh][None], (TS, JL, T))
                col = jnp.sum(jnp.where(pick, w, 0.0), axis=2, keepdims=True).reshape(TS * JL, 1)
                wb[hh] = jnp.broadcast_to(col, (TS * JL, T))

        def phase_a(si):
            b0, nb = SLOTS[si]
            keys = ki[b0 : b0 + nb].reshape(nb * T, T)
            part = None
            for hh in range(nh):
                xv = dot_nt(iq[hh], keys)
                wm = jnp.where(xv > 0.0, side_by_side([wb[hh]] * nb), 0.0)
                X[si][hh] = wm
                part = xv * wm if part is None else part + xv * wm
            LG[si][...] = jnp.sum(part.reshape(TS, JL, nb * T), axis=1)

        def phase_b(si):
            b0, nb = SLOTS[si]
            wait_all(RM[si], mr.at[si])
            total = M[si][mine, :]
            for r in range(PR):
                total = total + RM[si][r].astype(F32)
            live = side_by_side([mask[b0 + b] for b in range(nb)])
            g = jnp.where(live > 0.0, jnp.exp(LG[si][...] * index_scale - lse_col) - total * (1.0 / HEADS), 0.0)
            g = jnp.clip(g, -BIG, BIG)
            gv = jnp.broadcast_to(g[:, None, :], (TS, JL, nb * T)).reshape(TS * JL, nb * T)
            ac = acc.at[:, 0 : nb * T]
            ac[...] = gv

            @pl.loop(0, nh // 4)
            def _(i):
                for u in range(4):
                    hh = i * 4 + u
                    rows = pl.ds(pl.multiple_of(hh * TS * JL, TS * JL), TS * JL)
                    wt[rows, 0 : nb * T] = (ac[...] * X[si][hh]).astype(BF16)

            G[si][...] = jnp.dot(iqt[...], wt[:, 0 : nb * T], preferred_element_type=F32)
            GB[si][...] = G[si][...].astype(BF16)
            for r in FAR_FIRST:
                to = peer(r)
                toks = pl.ds(pl.multiple_of(to * TS, TS), TS)
                rcopy(GB[si].at[toks, :], RG[si].at[r - 1], gs.at[si], gr.at[si], (d, to)).start()

        def phase_c(si):
            b0, nb = SLOTS[si]
            wait_all(RG[si], gr.at[si])
            total = G[si][mine, :]
            for r in range(PR):
                total = total + RG[si][r].astype(F32)
            O[si][...] = total
            if si > 0:
                for b in range(nb):
                    k = hops[b0 + b]
                    rcopy(
                        O[si].at[:, b * T : (b + 1) * T], orecv.at[k - 1], osem, orsem, (seq(-k), h)
                    ).start()

        mass(0)
        relay_z(1)
        relay_z(2)
        relay_x(1)
        relay_z(3)
        relay_x(2)
        wait_d(1)
        mass(1)

        @pl.when(c == 0)
        def _():
            relay_z(4)

        send_index(range(NX, nh))
        relay_x(3)
        wait_d(2)
        mass(2)
        wait_d(3)
        mass(3)

        @pl.when(c == 0)
        def _():
            x_arrived(4)

        @pl.when(c == 1)
        def _():
            wait_recv(own_to_partner())

        mass(4)
        index_tables()
        phase_a(0)
        phase_b(0)
        phase_a(1)
        phase_b(1)
        phase_a(2)
        phase_b(2)
        phase_a(3)
        phase_a(4)
        phase_b(3)
        phase_b(4)
        phase_c(0)
        phase_c(1)
        phase_c(2)
        phase_c(3)
        phase_c(4)

        wait_all(orecv, orsem)
        total = O[0][...]
        for k in range(HOPS - 1):
            total = total + orecv[k]
        fin[mine, :] = total * index_scale
        for r in FAR_FIRST:
            rcopy(fin.at[mine, :], fin.at[mine, :], as_, ar, (d, peer(r))).start()
        wait_all(fin.at[0 : PR * TS, :], ar)
        out_ref[...] = fin[...].T

        for j in (1, 2, 3):
            for cp in zcopies(j) + x_copies(j, 0) + x_copies(j, 1) + d_copies(j, 0) + d_copies(j, 1):
                cp.wait_send()

        @pl.when(c == 1)
        def _():
            for cp in zcopies(4):
                cp.wait_send()

        @pl.when(c == 0)
        def _():
            for cp in own_to_partner() + x_copies(4, 0) + x_copies(4, 1):
                cp.wait_send()

        wait_all(iq.at[0:PR], iqs)
        wait_all(iw.at[0:PR], ws)
        for si in range(5):
            wait_all(RM[si], ms.at[si])
            wait_all(RG[si], gs.at[si])
        wait_all(orecv, osem)
        wait_all(fin.at[0 : PR * TS, :], as_)

    def slots(make):
        return [make(nb) for _, nb in SLOTS]

    dma = pltpu.SemaphoreType.DMA
    scratch = [
        pltpu.VMEM((HL, C, T), BF16),
        pltpu.VMEM((HL, T, C + 64), BF16),
        pltpu.VMEM((8, C, T), BF16),
        pltpu.VMEM((8, T, T), BF16),
        pltpu.VMEM((HL, T), F32),
        pltpu.VMEM((nh, TS * JL, T), BF16),
        pltpu.VMEM((T, nh * TS * JL), BF16),
        pltpu.VMEM((nh, JL, T), F32),
        pltpu.VMEM((nh, TS * JL, T), F32),
        pltpu.VMEM((1, T), F32),
        pltpu.VMEM((1, nseq), jnp.int32),
        pltpu.VMEM((nseq, nseq), jnp.int32),
        pltpu.VMEM((8, TS, T), F32),
        pltpu.VMEM((TS * JL, 2 * T), F32),
        *slots(lambda nb: pltpu.VMEM((T, nb * T), F32)),
        *slots(lambda nb: pltpu.VMEM((PR, TS, nb * T), BF16)),
        *slots(lambda nb: pltpu.VMEM((nh, TS * JL, nb * T), F32)),
        *slots(lambda nb: pltpu.VMEM((TS, nb * T), F32)),
        pltpu.VMEM((nh * TS * JL, 2 * T), BF16),
        *slots(lambda nb: pltpu.VMEM((T, nb * T), F32)),
        *slots(lambda nb: pltpu.VMEM((PR, TS, nb * T), BF16)),
        *slots(lambda nb: pltpu.VMEM((TS, nb * T), F32)),
        pltpu.VMEM((HOPS - 1, TS, T), F32),
        pltpu.VMEM((T, T), F32),
        *slots(lambda nb: pltpu.VMEM((T, nb * T), BF16)),
        *slots(lambda nb: pltpu.VMEM((T, nb * T), BF16)),
        dma((9,)), dma((4, 2)), dma((4, 2)), dma((4, 2, 2)), dma((4, 2, 2)), dma((4, 2, 2)), dma((4, 2, 2)),
        dma, dma, dma, dma, dma((5,)), dma((5,)), dma((5,)), dma((5,)), dma, dma, dma, dma,
    ]
    return kernel, scratch


def solution(mesh):
    nseq, nh = mesh.shape["seq"], mesh.shape["head"]
    kernel, scratch = make_kernel(nseq, nh)

    def local(q_main, latent_keys, lse_main, index_queries, index_weights, index_keys, lse_index, slab_order, block_live):
        return pl.pallas_call(
            kernel,
            out_shape=pltpu.VMEM(index_keys.shape, F32),
            in_specs=[pl.BlockSpec(memory_space=pltpu.HBM)] * 9,
            out_specs=pl.BlockSpec(memory_space=pltpu.VMEM),
            scratch_shapes=scratch,
            compiler_params=pltpu.CompilerParams(
                collective_id=0, has_side_effects=True, vmem_limit_bytes=60 * 2**20
            ),
        )(
            q_main.transpose(1, 2, 0),
            latent_keys.T,
            lse_main.T,
            index_queries.reshape(-1, index_queries.shape[2]),
            index_weights.T,
            index_keys,
            lse_index.reshape(1, -1),
            slab_order.reshape(1, -1),
            block_live,
        )

    placed = (
        P("seq", "head", None), P("seq", None), P("seq", "head"), P("seq", "head", None), P("seq", "head"),
        P("seq", None), P("seq"), P(), P(),
    )
    return jax.shard_map(local, mesh=mesh, in_specs=placed, out_specs=P("seq", None), check_vma=False)
```

time: 64.3 us -> 50.8 us (0.79)
  Pallas kernels: 62.7 us -> 50 us
  local copies, waits for them, and re-layouts: 1.47 us -> 0.63 us
    pallas_call x1, Pallas kernels: 62.7 us -> 50 us  [local(): pl.pallas_call(kernel, out_shape=pltpu.VMEM(index_keys.shape, F32), in_sp...]
    unnamed x1, local copies, waits for them, and re-layouts: 1.47 us -> 0.63 us
where the time goes in v2:
time: 50.8 us; the launch traced here: 50.6 us
  Pallas kernels  50 us (98%)
  local copies, waits for them, and re-layouts  0.63 us (1%)
    pallas_call x1, Pallas kernels, local(): pl.pallas_call(kernel, out_shape=pltpu.VMEM(index_keys.shape, F32), in_sp...  50 us

profile of v2, /device:TPU:1, one launch (start us, length us, event | category | flops | bytes accessed | tf_op | source)
XLA Modules:
  0.0 50.6 jit_solution(14220784603230477521)
XLA Ops:
  0.0 50.0 %shard_map.91 = f32[128,128]{1,0:T(8,128)S(1)} custom-call(bf16[16,576,128]{2,1,0:T(8,128)(2,1)} %bitcast.7, bf16[576,128]{1,0:T(8,128)(2,1)} %bitcast.9, f32[16,128]{1,0:T(8,128)} %bitcast.10, bf16[1024,128]{1,0:T(8,128)(2,1)} %bitcast.8, f32[8,128]{1,0:T(8,128)} %bitcast.11, bf16[128,128]{1,0:T(8,128)(2,1)} %ik_hbm.1, f32[1,128]{1,0:T(1,128)} %bitcast.12, ...), custom_call_target="tpu_custom_call" | custom-call | tf_op jit(solution)/shard_map/pallas_call | solution.py:445
  50.0 0.6 %copy.11 = f32[128,128]{1,0:T(8,128)} copy(f32[128,128]{1,0:T(8,128)S(1)} %shard_map.91) | data formatting | bytes 131072

commit v3 on v2

--- a/solution.py
+++ b/solution.py
@@ -34,6 +34,8 @@
     HALF, QUART = (C // 2, T // 2), (C // 4, T // 4)
     index_scale = 1.0 / 128.0**0.5
     GH = 4
+    HROWS = C // 2 + T // 2
+    LROWS = 2 * HL + TS * JL + 2 * JL
     FAR_FIRST = sorted(range(1, nh), key=lambda r: -2 * (r // NX) - min(r % NX, NX - r % NX))
     SLOTS = ((0, 1), (1, 2), (3, 2), (5, 2), (7, 1))
 
@@ -46,7 +48,7 @@
         g0, g1, g2, g3, g4, h0, h1, h2, h3, h4,
         o0, o1, o2, o3, o4, orecv, fin,
         mb0, mb1, mb2, mb3, mb4, gb0, gb1, gb2, gb3, gb4,
-        loc, zs, zr, xs, xr, ds, dr, iqs, iqr, ws, wr, ms, mr, gs, gr, osem, orsem, as_, ar,
+        loc, ks, zr, xr, dr, iqr, ws, wr, ms, mr, gr, osem, orsem, as_, ar,
     ):
         M = (m0, m1, m2, m3, m4)
         RM = (r0, r1, r2, r3, r4)
@@ -64,6 +66,9 @@
         yh = h - x
         odd, high = lax.rem(x, 2), x // 2
 
+        def wait_all(ref, sem):
+            pltpu.make_async_copy(ref, ref, sem).wait()
+
         def seq(offset):
             return lax.rem(d + offset + nseq, nseq)
 
@@ -72,13 +77,6 @@
 
         def xpeer(step):
             return yh + lax.rem(x + step, NX)
-
-        barrier = pltpu.get_barrier_semaphore()
-        for r in range(1, nh):
-            pl.semaphore_signal(barrier, inc=1, device_id=(d, peer(r)), device_id_type=MESH)
-        for k in range(1, HOPS):
-            pl.semaphore_signal(barrier, inc=1, device_id=(seq(k), h), device_id_type=MESH)
-            pl.semaphore_signal(barrier, inc=1, device_id=(seq(-k), h), device_id_type=MESH)
 
         mine = pl.ds(pl.multiple_of(h * TS, TS), TS)
         my_rows = pl.ds(pl.multiple_of(h * TS * JL, TS * JL), TS * JL)
@@ -86,16 +84,30 @@
             pltpu.make_async_copy(lat_hbm, kl.at[0], loc.at[0]),
             pltpu.make_async_copy(q_hbm, q, loc.at[1]),
             pltpu.make_async_copy(lse_hbm, lse, loc.at[2]),
-            pltpu.make_async_copy(ik_hbm, ki.at[0], loc.at[3]),
-            pltpu.make_async_copy(iq_hbm.at[my_rows, :], iq.at[PR], loc.at[4]),
-            pltpu.make_async_copy(iw_hbm, iw.at[PR], loc.at[5]),
-            pltpu.make_async_copy(lsei_hbm, lsei, loc.at[6]),
-            pltpu.make_async_copy(order_hbm, order, loc.at[7]),
-            pltpu.make_async_copy(blive_hbm, blive, loc.at[8]),
+            pltpu.make_async_copy(ik_hbm, ki.at[0], loc.at[0]),
+            pltpu.make_async_copy(iq_hbm.at[my_rows, :], iq.at[PR], loc.at[2]),
+            pltpu.make_async_copy(iw_hbm, iw.at[PR], loc.at[2]),
+            pltpu.make_async_copy(lsei_hbm, lsei, loc.at[3]),
+            pltpu.make_async_copy(order_hbm, order, loc.at[4]),
+            pltpu.make_async_copy(blive_hbm, blive, loc.at[5]),
         ]
-        for cp in locals_:
-            cp.start()
-        pl.semaphore_wait(barrier, PR + 2 * (HOPS - 1))
+        barrier = pltpu.get_barrier_semaphore()
+        for r in FAR_FIRST:
+            pl.semaphore_signal(barrier, inc=1, device_id=(d, peer(r)), device_id_type=MESH)
+        for k in range(HOPS - 1, 0, -1):
+            pl.semaphore_signal(barrier, inc=1, device_id=(seq(k), h), device_id_type=MESH)
+            pl.semaphore_signal(barrier, inc=1, device_id=(seq(-k), h), device_id_type=MESH)
+        for k in (-2, 2):
+            for step in (1, NX - 1):
+                pl.semaphore_signal(barrier, inc=1, device_id=(seq(k), xpeer(step)), device_id_type=MESH)
+
+        locals_[0].start()
+        locals_[3].start()
+
+        for i in (1, 2, 4, 5, 6, 7, 8):
+            locals_[i].start()
+        wait_all(kl.at[0:2, 0:HROWS, :], loc.at[0])
+        pl.semaphore_wait(barrier, PR + 2 * (HOPS - 1) + 4)
 
         def rcopy(src, dst, s, r, dev):
             return pltpu.make_async_remote_copy(
@@ -111,53 +123,57 @@
         whole = [pl.ds(0, C), pl.ds(0, T)]
         keys_at = (kl, ki)
 
-        def pieces(src, block, rows, s, r, dev):
+        def pieces(src, block, rows, r, dev):
             return [
-                rcopy(src[i].at[rows[i], :], keys_at[i].at[block, rows[i], :], s.at[i], r.at[i], dev)
+                rcopy(src[i].at[rows[i], :], keys_at[i].at[block, rows[i], :], ks, r, dev)
                 for i in range(2)
             ]
 
-        def kpieces(block, rows, s, r, dev):
-            return pieces((kl.at[block], ki.at[block]), block, rows, s, r, dev)
-
-        own_keys = (lat_hbm, ik_hbm)
+        def kpieces(block, rows, r, dev):
+            return pieces((kl.at[block], ki.at[block]), block, rows, r, dev)
+
+        own_keys = (kl.at[0], ki.at[0])
+
+        second = (kl.at[3 + c], ki.at[3 + c])
 
         def zcopies(j):
-            if j < 4:
-                return pieces(own_keys, 2 * j - 1 + c, own_half, zs.at[j - 1], zr.at[j - 1], (seq(2 * j), h))
-            return pieces(own_keys, 7, own_half, zs.at[3], zr.at[3], (seq(7), h))
+            return pieces(own_keys, 2 * j - 1 + c, own_half, zr.at[j - 1], (seq(2 * j), h))
+
+        def third_relay():
+            return pieces(second, 5 + c, own_half, zr.at[2], (seq(2), h))
+
+        def third_quarters(way):
+            return pieces(
+                second, 5 + c, own_quart, xr.at[2], (seq(2), xpeer((1, NX - 1)[way]))
+            )
+
+        def fourth_relay():
+            return pieces(second, 7, own_half, zr.at[3], (seq(3), h))
 
         def own_to_partner():
-            return pieces(own_keys, 7, whole, ds.at[3, 0], dr.at[3, 0], (seq(1), h))
+            return pieces(own_keys, 7, whole, dr.at[3], (seq(1), h))
 
         def send_index(rs):
             for r in rs:
                 to = peer(r)
                 rows = pl.ds(pl.multiple_of(to * TS * JL, TS * JL), TS * JL)
-                rcopy(iq_hbm.at[rows, :], iq.at[r - 1], iqs, iqr, (d, to)).start()
+                rcopy(iq_hbm.at[rows, :], iq.at[r - 1], ms, iqr, (d, to)).start()
                 rcopy(iw_hbm, iw.at[r - 1], ws, wr, (d, to)).start()
 
         def far_sends():
-            for cp in zcopies(3):
-                cp.start()
-
-            @pl.when(c == 1)
-            def _():
-                for cp in zcopies(4):
-                    cp.start()
-
             @pl.when(c == 0)
             def _():
                 for cp in own_to_partner():
                     cp.start()
 
         send_index(range(1, NX))
-        for j in (1, 2):
+        for j in (2, 1):
             for cp in zcopies(j):
                 cp.start()
 
-        for cp in locals_:
-            cp.wait()
+        for i in (1, 6, 7, 8):
+            locals_[i].wait()
+        wait_all(kl.at[0, 0:LROWS, :], loc.at[2])
 
         @pl.loop(0, HL // 4)
         def _(i):
@@ -213,39 +229,41 @@
             for r in FAR_FIRST:
                 to = peer(r)
                 toks = pl.ds(pl.multiple_of(to * TS, TS), TS)
-                rcopy(MB[si].at[toks, :], RM[si].at[r - 1], ms.at[si], mr.at[si], (d, to)).start()
-
-        def wait_all(ref, sem):
-            pltpu.make_async_copy(ref, ref, sem).wait()
-
-        def wait_recv(copies):
-            for cp in copies:
-                cp.wait_recv()
+                rcopy(MB[si].at[toks, :], RM[si].at[r - 1], ms, mr.at[si], (d, to)).start()
 
         def block_of(j):
             return 2 * j - 1 + c if j < 4 else 7
 
         def x_copies(j, way):
             return kpieces(
-                block_of(j), own_quart, xs.at[j - 1, way], xr.at[j - 1, way], (d, xpeer((1, NX - 1)[way]))
+                block_of(j), own_quart, xr.at[j - 1], (d, xpeer((1, NX - 1)[way]))
             )
 
         def d_copies(j, part):
             rows = (own_half, other_half)[part]
-            return kpieces(2 * j - 1 + c, rows, ds.at[j - 1, part], dr.at[j - 1, part], (d + 1 - 2 * c, h))
+            return kpieces(2 * j - 1 + c, rows, dr.at[j - 1], (d + 1 - 2 * c, h))
 
         def relay_z(j):
-            wait_recv(kpieces(block_of(j), own_half, zs.at[j - 1], zr.at[j - 1], (d, h)))
-            for way in (0, 1):
-                for cp in x_copies(j, way):
+            wait_all(kl.at[0, 0:HROWS, :], zr.at[j - 1])
+            if j == 2:
+                for cp in third_relay() + third_quarters(0) + third_quarters(1):
                     cp.start()
+
+                @pl.when(c == 1)
+                def _():
+                    for cp in fourth_relay():
+                        cp.start()
+
+            if j != 3:
+                for way in (0, 1):
+                    for cp in x_copies(j, way):
+                        cp.start()
             if j < 4:
                 for cp in d_copies(j, 0):
                     cp.start()
 
         def x_arrived(j):
-            for way in (0, 1):
-                wait_recv(x_copies(j, way))
+            wait_all(kl.at[0, 0:HROWS, :], xr.at[j - 1])
 
         def relay_x(j):
             x_arrived(j)
@@ -253,9 +271,7 @@
                 cp.start()
 
         def wait_d(j):
-            for part in (0, 1):
-                rows = (own_half, other_half)[part]
-                wait_recv(kpieces(2 * j - c, rows, ds.at[j - 1, part], dr.at[j - 1, part], (d, h)))
+            wait_all(kl.at[0:2, 0:HROWS, :], dr.at[j - 1])
 
         def index_tables():
             wait_all(iq.at[0:PR], iqr)
@@ -291,22 +307,15 @@
             g = jnp.where(live > 0.0, jnp.exp(LG[si][...] * index_scale - lse_col) - total * (1.0 / HEADS), 0.0)
             g = jnp.clip(g, -BIG, BIG)
             gv = jnp.broadcast_to(g[:, None, :], (TS, JL, nb * T)).reshape(TS * JL, nb * T)
-            ac = acc.at[:, 0 : nb * T]
-            ac[...] = gv
-
-            @pl.loop(0, nh // 4)
-            def _(i):
-                for u in range(4):
-                    hh = i * 4 + u
-                    rows = pl.ds(pl.multiple_of(hh * TS * JL, TS * JL), TS * JL)
-                    wt[rows, 0 : nb * T] = (ac[...] * X[si][hh]).astype(BF16)
+            for hh in range(nh):
+                wt[hh * TS * JL : (hh + 1) * TS * JL, 0 : nb * T] = (gv * X[si][hh]).astype(BF16)
 
             G[si][...] = jnp.dot(iqt[...], wt[:, 0 : nb * T], preferred_element_type=F32)
             GB[si][...] = G[si][...].astype(BF16)
             for r in FAR_FIRST:
                 to = peer(r)
                 toks = pl.ds(pl.multiple_of(to * TS, TS), TS)
-                rcopy(GB[si].at[toks, :], RG[si].at[r - 1], gs.at[si], gr.at[si], (d, to)).start()
+                rcopy(GB[si].at[toks, :], RG[si].at[r - 1], ms, gr.at[si], (d, to)).start()
 
         def phase_c(si):
             b0, nb = SLOTS[si]
@@ -323,22 +332,22 @@
                     ).start()
 
         mass(0)
+        relay_z(2)
         relay_z(1)
-        relay_z(2)
+        relay_x(2)
+        send_index(reversed(range(NX, nh)))
         relay_x(1)
-        relay_z(3)
-        relay_x(2)
-        wait_d(1)
-        mass(1)
 
         @pl.when(c == 0)
         def _():
             relay_z(4)
 
-        send_index(range(NX, nh))
-        relay_x(3)
         wait_d(2)
         mass(2)
+        relay_z(3)
+        relay_x(3)
+        wait_d(1)
+        mass(1)
         wait_d(3)
         mass(3)
 
@@ -348,25 +357,25 @@
 
         @pl.when(c == 1)
         def _():
-            wait_recv(own_to_partner())
+            wait_d(4)
 
         mass(4)
         index_tables()
+        phase_a(2)
+        phase_b(2)
+        phase_a(1)
+        phase_b(1)
+        phase_a(3)
+        phase_b(3)
+        phase_a(4)
+        phase_b(4)
         phase_a(0)
         phase_b(0)
-        phase_a(1)
-        phase_b(1)
-        phase_a(2)
-        phase_b(2)
-        phase_a(3)
-        phase_a(4)
-        phase_b(3)
-        phase_b(4)
-        phase_c(0)
+        phase_c(2)
         phase_c(1)
-        phase_c(2)
         phase_c(3)
         phase_c(4)
+        phase_c(0)
 
         wait_all(orecv, orsem)
         total = O[0][...]
@@ -375,29 +384,20 @@
         fin[mine, :] = total * index_scale
         for r in FAR_FIRST:
             rcopy(fin.at[mine, :], fin.at[mine, :], as_, ar, (d, peer(r))).start()
+        @pl.when(c == 0)
+        def _():
+            wait_all(q.at[0:15, 0:HROWS, :], ks)
+
+        @pl.when(c == 1)
+        def _():
+            wait_all(q.at[0:13, 0:HROWS, :], ks)
+
+        wait_all(q.at[0:14, 0 : PR * (T + 2 * T) // 14, :], ms)
+        wait_all(iw.at[0:PR], ws)
+        wait_all(orecv, osem)
+
         wait_all(fin.at[0 : PR * TS, :], ar)
         out_ref[...] = fin[...].T
-
-        for j in (1, 2, 3):
-            for cp in zcopies(j) + x_copies(j, 0) + x_copies(j, 1) + d_copies(j, 0) + d_copies(j, 1):
-                cp.wait_send()
-
-        @pl.when(c == 1)
-        def _():
-            for cp in zcopies(4):
-                cp.wait_send()
-
-        @pl.when(c == 0)
-        def _():
-            for cp in own_to_partner() + x_copies(4, 0) + x_copies(4, 1):
-                cp.wait_send()
-
-        wait_all(iq.at[0:PR], iqs)
-        wait_all(iw.at[0:PR], ws)
-        for si in range(5):
-            wait_all(RM[si], ms.at[si])
-            wait_all(RG[si], gs.at[si])
-        wait_all(orecv, osem)
         wait_all(fin.at[0 : PR * TS, :], as_)
 
     def slots(make):
@@ -431,8 +431,8 @@
         pltpu.VMEM((T, T), F32),
         *slots(lambda nb: pltpu.VMEM((T, nb * T), BF16)),
         *slots(lambda nb: pltpu.VMEM((T, nb * T), BF16)),
-        dma((9,)), dma((4, 2)), dma((4, 2)), dma((4, 2, 2)), dma((4, 2, 2)), dma((4, 2, 2)), dma((4, 2, 2)),
-        dma, dma, dma, dma, dma((5,)), dma((5,)), dma((5,)), dma((5,)), dma, dma, dma, dma,
+        dma((6,)), dma, dma((4,)), dma((4,)), dma((4,)),
+        dma, dma, dma, dma, dma((5,)), dma((5,)), dma, dma, dma, dma,
     ]
     return kernel, scratch
 

time: 50.8 us -> 46.5 us (0.915)
  Pallas kernels: 50 us -> 45.7 us
    pallas_call x1, Pallas kernels: 50 us -> 45.7 us  [local(): pl.pallas_call(kernel, out_shape=pltpu.VMEM(index_keys.shape, F32), in_sp...]
where the time goes in v3:
time: 46.5 us; the launch traced here: 46.3 us
  Pallas kernels  45.7 us (98%)
  local copies, waits for them, and re-layouts  0.63 us (1%)
    pallas_call x1, Pallas kernels, local(): pl.pallas_call(kernel, out_shape=pltpu.VMEM(index_keys.shape, F32), in_sp...  45.7 us

profile of v3, /device:TPU:1, one launch (start us, length us, event | category | flops | bytes accessed | tf_op | source)
XLA Modules:
  0.0 46.3 jit_solution(12301560415548277546)
XLA Ops:
  0.0 45.7 %shard_map.91 = f32[128,128]{1,0:T(8,128)S(1)} custom-call(bf16[16,576,128]{2,1,0:T(8,128)(2,1)} %bitcast.7, bf16[576,128]{1,0:T(8,128)(2,1)} %bitcast.9, f32[16,128]{1,0:T(8,128)} %bitcast.10, bf16[1024,128]{1,0:T(8,128)(2,1)} %bitcast.8, f32[8,128]{1,0:T(8,128)} %bitcast.11, bf16[128,128]{1,0:T(8,128)(2,1)} %ik_hbm.1, f32[1,128]{1,0:T(1,128)} %bitcast.12, ...), custom_call_target="tpu_custom_call" | custom-call | tf_op jit(solution)/shard_map/pallas_call | solution.py:445
  45.7 0.6 %copy.11 = f32[128,128]{1,0:T(8,128)} copy(f32[128,128]{1,0:T(8,128)S(1)} %shard_map.91) | data formatting | bytes 131072
